TPU v7x, 32 devices: a whole 2x2x4 slice. The times are simulated.
32 devices in a mesh: expert: 4 (over y, x), dp: 8 (over z, core).
Axes of the slice: x: 2, y: 2, z: 4, core: 2. Of those that a mesh axis runs over, the one named last changes fastest.
Arguments:
- acts: bfloat16 [32, 4, 16, 3584], P(('expert', 'dp')), may hold values from -6 to 6
- grad_out: bfloat16 [32, 4, 16, 1024], P(('expert', 'dp')), may hold values from -0.375 to 0.375
- routing_counts: int32 [32, 4], P(('expert', 'dp')), may hold values from 1 to 16, as said below
- left_basis: bfloat16 [4, 3584, 3584], P('expert', 'dp'), may hold values from -1 to 1, as said below
- right_basis: bfloat16 [4, 1024, 1024], P('expert'), may hold values from -1 to 1, as said below
- first_moment: float32 [4, 3584, 1024], P('expert', 'dp'), may hold values from -3 to 3
- second_moment: float32 [4, 3584, 1024], P('expert', 'dp'), may hold values from 0.05 to 2000
Outputs:
- step_delta: bfloat16 [4, 3584, 1024], P('expert', 'dp')
- first_out: float32 [4, 3584, 1024], P('expert', 'dp')
- second_out: float32 [4, 3584, 1024], P('expert', 'dp')
- expert_rms: float32 [4], P('expert')
Inputs may be any that keep to these rules, and one draw needn't show every extreme that they name: Slot s of shard i for expert e carries a routed token when s < routing_counts[i, e]; the other slots hold leftover values that belong to no token. In every shard some expert has all 16 slots live. `left_basis`: each expert's block is an orthogonal matrix rounded to bfloat16. `right_basis`: each expert's block is an orthogonal matrix rounded to bfloat16.
All inputs are finite; a program needn't handle non-finite values.
Results may differ from a plain program's by a relative error of at most 0.013.
Values may be sent and summed in bfloat16 or wider, within the bound.
A program may use at most 64 MiB of HBM per device.

v0:
```python
import jax
import jax.numpy as jnp
from jax import lax
from jax.sharding import PartitionSpec as P

BETA_ONE = 0.9
BETA_TWO = 0.95
EPS_DIVIDE = 1e-08
EPS_MEAN = 1e-06


def local(acts, grad_out, routing_counts, left_basis, right_basis, first_moment, second_moment):
    slot_count = acts.shape[2]
    slot_index = lax.broadcasted_iota(jnp.int32, routing_counts.shape + (slot_count,), 2)
    live_slots = (slot_index < routing_counts[:, :, None])[..., None]
    acts_live = jnp.where(live_slots, acts, jnp.zeros((), jnp.bfloat16))
    grads_live = jnp.where(live_slots, grad_out, jnp.zeros((), jnp.bfloat16))
    came_acts, came_grads = (
        lax.all_to_all(acts_live, "expert", split_axis=1, concat_axis=0, tiled=True),
        lax.all_to_all(grads_live, "expert", split_axis=1, concat_axis=0, tiled=True),
    )
    model_width = came_acts.shape[-1]
    hidden_width = came_grads.shape[-1]
    column_slabs = lax.all_to_all(came_acts, "dp", split_axis=3, concat_axis=0, tiled=True)
    grad_slabs = lax.all_gather(came_grads, "dp", axis=0, tiled=True)
    source_count = lax.axis_size("dp")
    column_slabs = column_slabs.reshape(source_count, -1, column_slabs.shape[-1])
    grad_slabs = grad_slabs.reshape(source_count, -1, hidden_width)
    partials = jnp.einsum(
        "stk,stf->skf", column_slabs, grad_slabs, preferred_element_type=jnp.float32
    )
    partials = lax.optimization_barrier(partials.astype(jnp.bfloat16))
    summed = jnp.sum(partials.astype(jnp.float32), axis=0)
    gradient = summed.astype(jnp.bfloat16)
    right_block = right_basis[0]
    left_rows = left_basis[0]
    right_turned = jnp.dot(gradient, right_block, preferred_element_type=jnp.float32).astype(
        jnp.bfloat16
    )
    basis_columns = left_rows
    rotated = lax.psum_scatter(
        jnp.einsum(
            "kc,kf->cf", basis_columns, right_turned, preferred_element_type=jnp.float32
        ).astype(jnp.bfloat16),
        "dp",
        scatter_dimension=0,
        tiled=True,
    ).astype(jnp.float32)
    first_new = BETA_ONE * first_moment[0] + (1.0 - BETA_ONE) * rotated
    second_new = BETA_TWO * second_moment[0] + (1.0 - BETA_TWO) * rotated * rotated
    direction = (first_new / (jnp.sqrt(second_new) + EPS_DIVIDE)).astype(jnp.bfloat16)
    restored = jnp.einsum(
        "kg,fg->kf", direction, right_block, preferred_element_type=jnp.float32
    ).astype(jnp.bfloat16)
    basis_columns = left_rows
    update = jnp.dot(
        basis_columns,
        lax.all_gather(restored, "dp", axis=0, tiled=True),
        preferred_element_type=jnp.float32,
    )
    squares = jnp.sum(update * update)
    cell_total = float(model_width * hidden_width)
    total_squares = lax.psum(squares, "dp")
    own_norm = jnp.sqrt(total_squares / cell_total + EPS_MEAN)
    norm_total = lax.psum(own_norm, "expert")
    mean_norm = norm_total / lax.axis_size("expert")
    step_delta = (-update / jnp.maximum(own_norm, mean_norm)).astype(jnp.bfloat16)
    return (step_delta[None], first_new[None], second_new[None], own_norm.reshape(1))


def solution(mesh):
    in_specs = (
        P(("expert", "dp"), None, None, None),
        P(("expert", "dp"), None, None, None),
        P(("expert", "dp"), None),
        P("expert", "dp", None),
        P("expert", None, None),
        P("expert", "dp", None),
        P("expert", "dp", None),
    )
    out_specs = (
        P("expert", "dp", None),
        P("expert", "dp", None),
        P("expert", "dp", None),
        P("expert"),
    )
    return jax.shard_map(local, mesh=mesh, in_specs=in_specs, out_specs=out_specs, check_vma=False)
```

profile of v0, /device:TPU:0, one launch (start us, length us, event | category | flops | bytes accessed | tf_op | source)
XLA Modules:
  0.0 312.0 jit_solution(15991708466216752481)
XLA Ops:
  9.1 10.1 %all_to_all.39 = bf16[1,4,16,1024]{3,2,0,1:T(8,128)(2,1)} all-to-all(bf16[1,4,16,1024]{3,2,0,1:T(8,128)(2,1)S(1)} %bitcast_select_fusion.1), channel_id=1, replica_groups=mesh['expert'=4,'dp'=8] {'expert'}, dimensions={1} | all-to-all | bytes 262144 | tf_op jit(solution)/shard_map/all_to_all | solution.py:20
  20.5 10.0 %all_to_all.40 = bf16[1,4,16,3584]{3,2,0,1:T(8,128)(2,1)} all-to-all(bf16[1,4,16,3584]{3,2,0,1:T(8,128)(2,1)S(1)} %bitcast_select_fusion), channel_id=1, replica_groups=mesh['expert'=4,'dp'=8] {'expert'}, dimensions={1} | all-to-all | bytes 917504 | tf_op jit(solution)/shard_map/all_to_all | solution.py:19
  30.5 5.3 %copy.31 = bf16[4,1,16,3584]{2,0,1,3:T(4,128)(2,1)} copy(bf16[4,1,16,3584]{3,2,0,1:T(8,128)(2,1)} %bitcast.64) | data formatting | bytes 917504 | tf_op jit(solution)/shard_map/all_to_all | solution.py:19
  35.8 6.0 %reshape.63 = bf16[8,2,14336]{2,1,0:T(2,128)(2,1)} reshape(bf16[3584,1,4,16]{3,2,1,0:T(4,128)(2,1)} %bitcast.60) | data formatting | bytes 917504
  41.7 18.9 %all_to_all.41 = bf16[8,2,14336]{2,1,0:T(2,128)(2,1)} all-to-all(bf16[8,2,14336]{2,1,0:T(2,128)(2,1)} %reshape.63), channel_id=1, replica_groups=mesh['expert'=4,'dp'=8] {'dp'}, dimensions={0} | all-to-all | bytes 917504 | tf_op jit(solution)/shard_map/all_to_all | solution.py:24
  60.7 5.1 %reshape.64 = bf16[3584,1,4,16]{3,2,1,0:T(4,128)(2,1)} reshape(bf16[8,2,14336]{2,1,0:T(2,128)(2,1)} %all_to_all.41) | data formatting | bytes 917504
  65.7 5.1 %copy.38 = bf16[4,1,16,8,448]{4,3,2,0,1:T(8,128)(2,1)} copy(bf16[4,1,16,8,448]{2,0,4,3,1:T(4,128)(2,1)} %bitcast.61) | data formatting | bytes 917504 | tf_op jit(solution)/shard_map/all_to_all | solution.py:24
  72.8 6.5 %convolution_convert_fusion.1 = bf16[8,448,1024]{2,1,0:T(8,128)(2,1)} fusion(bf16[8,64,448]{2,1,0:T(8,128)(2,1)} %bitcast.62, bf16[8,64,1024]{2,1,0:T(8,128)(2,1)} %bitcast.65), kind=kOutput, calls=%fused_computation.2 | convolution fusion | flops 473432064 | bytes 8847360 | tf_op jit(solution)/shard_map/stk,stf->skf/dot_general | solution.py:29
  79.3 6.0 %reduce_sum.21 = bf16[448,1024]{1,0:T(8,128)(2,1)} reduce(bf16[8,448,1024]{2,1,0:T(8,128)(2,1)} %convolution_convert_fusion.1, bf16[]{:T(256)} %constant.4.clone.1), dimensions={0}, to_apply=%region_0.1 | reduce | flops 3211264 | bytes 8257538 | tf_op jit(solution)/shard_map/reduce_sum | solution.py:33
  85.3 9.9 %fusion = bf16[3584,1024]{0,1:T(8,128)(2,1)} fusion(bf16[1,448,3584]{2,1,0:T(8,128)(2,1)S(1)} %copy-done, bf16[448,1024]{1,0:T(8,128)(2,1)} %reduce_sum.21, bf16[1,1024,1024]{2,1,0:T(8,128)(2,1)} %param.11), kind=kOutput, calls=%fused_computation.1 | convolution fusion | flops 4231987200 | bytes 13565952 | tf_op jit(solution)/shard_map/kc,kf->cf/dot_general | solution.py:42
  95.2 10.4 %copy.39 = bf16[3584,1024]{1,0:T(8,128)(2,1)} copy(bf16[3584,1024]{0,1:T(8,128)(2,1)} %fusion) | data formatting | bytes 14680064
  105.9 2.9 copy.29
  108.8 3.0 copy.35
  111.8 70.9 %reduce-scatter.4.cloned.1.call-done = bf16[448,1024]{1,0:T(8,128)(2,1)} async-done(((bf16[3584,1024]{1,0:T(8,128)(2,1)}), bf16[448,1024]{1,0:T(8,128)(2,1)}) %reduce-scatter.4.cloned.1.call-update) | async-done | bytes 917520
  182.6 2.2 copy.40
  184.9 6.4 %fusion.13 = bf16[448,1024]{1,0:T(8,128)(2,1)} fusion(bf16[1,1024,1024]{2,1,0:T(8,128)(2,1)} %param.11, bf16[448,1024]{0,1:T(8,128)(2,1)} %copy.40, f32[1,448,1024]{1,2,0:T(8,128)} %copy.29, f32[1,448,1024]{1,2,0:T(8,128)} %copy.35), kind=kOutput, calls=%fused_computation.18 | convolution fusion | flops 945029120 | bytes 7602176 | tf_op jit(solution)/shard_map/kg,fg->kf/dot_general | solution.py:52
  191.3 5.4 %fusion.17 = (f32[1,448,1024]{1,2,0:T(8,128)}, f32[1,448,1024]{1,2,0:T(8,128)}) fusion(bf16[448,1024]{0,1:T(8,128)(2,1)} %copy.40, f32[1,448,1024]{1,2,0:T(8,128)} %copy.35, f32[1,448,1024]{1,2,0:T(8,128)} %copy.29), kind=kLoop, calls=%fused_computation.20 | loop fusion | flops 3670016 | bytes 8257536 | tf_op jit(solution)/shard_map/broadcast_in_dim | solution.py:68
  196.7 3.0 copy.36
  199.7 63.6 %all-gather.4.cloned.1.call-done = bf16[3584,1024]{1,0:T(8,128)(2,1)} async-done(((bf16[448,1024]{1,0:T(8,128)(2,1)}), bf16[3584,1024]{1,0:T(8,128)(2,1)}) %all-gather.4.cloned.1.call-update) | async-done | bytes 7340048 | tf_op jit(solution)/shard_map/all_gather | solution.py:58
  263.3 8.4 %multiply_reduce_fusion = (f32[]{:T(128)}, f32[1024,448]{0,1:T(8,128)}) fusion(bf16[3584,1024]{1,0:T(8,128)(2,1)} %all-gather.4.cloned.1.call-done, bf16[1,448,3584]{2,1,0:T(8,128)(2,1)S(1)} %copy-done), kind=kOutput, calls=%fused_computation.16 | convolution fusion | flops 3289251840 | bytes 12386308 | tf_op jit(solution)/shard_map/dot_general | solution.py:56
  271.6 14.7 %psum.14 = f32[]{:T(128)} all-reduce(f32[]{:T(128)} %get-tuple-element.22), channel_id=1, replica_groups=mesh['expert'=4,'dp'=8] {'dp'}, use_global_device_ids=true, to_apply=%region_3.4 | all-reduce | flops 1 | bytes 8 | tf_op jit(solution)/shard_map/psum | solution.py:63
  287.0 2.8 copy.37
  289.8 11.2 %psum.15 = f32[]{:T(128)} all-reduce(f32[]{:T(128)} %sqrt.7), channel_id=1, replica_groups=mesh['expert'=4,'dp'=8] {'expert'}, use_global_device_ids=true, to_apply=%region_4.5 | all-reduce | flops 1 | bytes 8 | tf_op jit(solution)/shard_map/psum | solution.py:65
  301.7 2.6 fusion.18
  (13 shorter events, 5.4 us)
Async XLA Ops:
  7.2 78.1 %copy-start = (bf16[1,448,3584]{2,1,0:T(8,128)(2,1)S(1)}, bf16[1,448,3584]{2,1,0:T(8,128)(2,1)}, u32[]{:S(2)}) copy-start(bf16[1,448,3584]{2,1,0:T(8,128)(2,1)} %param.10) | copy-start | bytes 9633796
  7.2 65.7 %all-gather.6.cloned.1.call-start = ((), (), s32[]{:S(2)}) async-start(), calls=%async_computation.5 | async-start | bytes 1179648 | tf_op jit(solution)/shard_map/all_gather | solution.py:25
  19.3 163.3 %reduce-scatter.4.cloned.1.call-start = ((), (), s32[]{:S(2)}) async-start(), calls=%async_computation.6 | async-start | bytes 8257536
  105.6 157.7 %all-gather.4.cloned.1.call-start = ((), (), s32[]{:S(2)}) async-start(), calls=%async_computation.4 | async-start | bytes 8257536 | tf_op jit(solution)/shard_map/all_gather | solution.py:58
Sparse Core Ops, SparseCore 0:
  19.4 21.7 all-gather.5
  105.7 76.8 reduce-scatter.3
  191.4 71.7 all-gather.3
where the time goes:
time: 313 us; the launch traced here: 312 us
  waiting for transfers between devices  134 us (43%)
  blocking collectives  65 us (21%)
  local copies, waits for them, and re-layouts  47.8 us (15%)
  matrix products  31.1 us (10%)
  other arithmetic  17.1 us (5%)
  between operations  16.3 us (5%)
    unnamed x4, waiting for transfers between devices  70.9 us
    all_gather x1, waiting for transfers between devices, local(): lax.all_gather(restored, 'dp', axis=0, tiled=True)  63.6 us
    unnamed x10, local copies, waits for them, and re-layouts  35.4 us
    all_to_all x1, blocking collectives, local(): lax.all_to_all(came_acts, 'dp', split_axis=3, concat_axis=0, tiled=True)  18.9 us
    psum x1, blocking collectives, local(): total_squares = lax.psum(squares, 'dp')  14.7 us
    psum x1, blocking collectives, local(): norm_total = lax.psum(own_norm, 'expert')  11.2 us
    all_to_all x1, blocking collectives, local(): lax.all_to_all(grads_live, 'expert', split_axis=1, concat_axis=0, tiled=T...  10.1 us
    all_to_all x1, blocking collectives, local(): lax.all_to_all(acts_live, 'expert', split_axis=1, concat_axis=0, tiled=True)  10 us
  transfers between devices with their start and end apart: 3, of which 2 were waited for; matrix products, arithmetic and copies ran while one was open for 12% of the time, Pallas kernels for 0%

commit v1 on v0

--- a/solution.py
+++ b/solution.py
@@ -1,6 +1,10 @@
+import functools
+
 import jax
 import jax.numpy as jnp
 from jax import lax
+from jax.experimental import pallas as pl
+from jax.experimental.pallas import tpu as pltpu
 from jax.sharding import PartitionSpec as P
 
 BETA_ONE = 0.9
@@ -68,6 +72,438 @@
     return (step_delta[None], first_new[None], second_new[None], own_norm.reshape(1))
 
 
+CORES = 2
+PIECES = 2
+TILE = 256
+MESH = pl.DeviceIdType.MESH
+VMEM_BYTES = 60 * 1024 * 1024
+
+
+def remote(src, dst, send_sem, recv_sem, expert, dp):
+    return pltpu.make_async_remote_copy(
+        src_ref=src,
+        dst_ref=dst,
+        send_sem=send_sem,
+        recv_sem=recv_sem,
+        device_id=(expert, dp),
+        device_id_type=MESH,
+    )
+
+
+def greet_all(experts, dps, expert, dp):
+    barrier = pltpu.get_barrier_semaphore()
+    for offset in range(1, experts * dps):
+        target = (
+            lax.rem(expert + offset // dps, experts),
+            lax.rem(dp + offset % dps, dps),
+        )
+        pl.semaphore_signal(barrier, inc=1, device_id=target, device_id_type=MESH)
+    pl.semaphore_wait(barrier, experts * dps - 1)
+
+
+def exchange_kernel(
+    experts, chips, acts, acts_out, acts_send, acts_recv, own_sem
+):
+    dps = chips * CORES
+    expert, dp = lax.axis_index("expert"), lax.axis_index("dp")
+    chip, core = dp // CORES, lax.rem(dp, CORES)
+    greet_all(experts, dps, expert, dp)
+    own_acts = pltpu.make_async_copy(
+        acts.at[dp, expert], acts_out.at[core, expert, chip], own_sem
+    )
+    own_acts.start()
+    acts_copies = []
+    for chip_offset in reversed(range(chips)):
+        to_chip = lax.rem(chip + chip_offset, chips)
+        for expert_offset in range(experts):
+            to_expert = lax.rem(expert + expert_offset, experts)
+            for core_offset in range(CORES):
+                if chip_offset + expert_offset + core_offset > 0:
+                    to_dp = to_chip * CORES + lax.rem(core + core_offset, CORES)
+                    index = (chip_offset * experts + expert_offset) * CORES + core_offset
+                    copy = remote(
+                        acts.at[to_dp, to_expert], acts_out.at[core, expert, chip],
+                        acts_send.at[index], acts_recv.at[index], to_expert, to_dp,
+                    )
+                    copy.start()
+                    acts_copies.append(copy)
+    own_acts.wait()
+    for copy in acts_copies:
+        copy.wait()
+
+
+def exchange(acts, experts, chips):
+    slots, width = acts.shape[2:]
+    count = experts * chips
+    vmem = pl.BlockSpec(memory_space=pltpu.VMEM)
+    dma = pltpu.SemaphoreType.DMA
+    return pl.pallas_call(
+        functools.partial(exchange_kernel, experts, chips),
+        out_shape=jax.ShapeDtypeStruct((CORES, experts, chips, slots, width), acts.dtype),
+        in_specs=[vmem],
+        out_specs=vmem,
+        scratch_shapes=[dma((count * CORES,)), dma((count * CORES,)), dma],
+        compiler_params=pltpu.CompilerParams(
+            collective_id=0, has_side_effects=True, vmem_limit_bytes=VMEM_BYTES
+        ),
+    )(acts)
+
+
+def reduce_kernel(
+    experts, chips, part, grads, out, grads_out, paired, held, came, total,
+    pair_send, pair_recv, send_sem, recv_sem,
+    grads_send, grads_recv, swap_send, swap_recv, own_sem,
+):
+    expert, dp = lax.axis_index("expert"), lax.axis_index("dp")
+    chip, core = dp // CORES, lax.rem(dp, CORES)
+    partner = chip * CORES + (1 - core)
+    rows = out.shape[0]
+    greet_all(experts, chips * CORES, expert, dp)
+
+    def block(index):
+        return part.at[pl.ds(pl.multiple_of(index * rows, 16), rows)]
+
+    pairs = {}
+    order = sorted(range(chips), key=lambda to: -abs(2 * to - chips + 1))
+    for to in order:
+        pairs[to] = remote(
+            block(to * CORES + 1 - core), paired.at[to],
+            pair_send.at[to], pair_recv.at[to], expert, partner,
+        )
+        pairs[to].start()
+
+    own_grads = pltpu.make_async_copy(
+        grads.at[expert], grads_out.at[core, expert, chip], own_sem
+    )
+    own_grads.start()
+    grads_copies = []
+    for chip_offset in reversed(range(chips)):
+        to_chip = lax.rem(chip + chip_offset, chips)
+        for expert_offset in range(experts):
+            to_expert = lax.rem(expert + expert_offset, experts)
+            if chip_offset + expert_offset > 0:
+                index = chip_offset * experts + expert_offset
+                copy = remote(
+                    grads.at[to_expert], grads_out.at[core, expert, chip],
+                    grads_send.at[index], grads_recv.at[index],
+                    to_expert, to_chip * CORES + core,
+                )
+                copy.start()
+                grads_copies.append(copy)
+
+    def line_copy(way, to):
+        step = CORES if way == 0 else -CORES
+        return remote(
+            held.at[to], came.at[way, to], send_sem.at[way, to], recv_sem.at[way, to],
+            expert, dp + step,
+        )
+
+    def both(to):
+        mine = block(to * CORES + core)[...].astype(jnp.float32)
+        return mine + paired[to].astype(jnp.float32)
+
+    def hand_on(way, to):
+        first = (chip == 0) if way == 0 else (chip == chips - 1)
+        before = (chip < to) if way == 0 else (chip > to)
+
+        @pl.when(jnp.logical_and(before, first))
+        def _():
+            pairs[to].wait_recv()
+            held[to] = both(to).astype(jnp.bfloat16)
+            line_copy(way, to).start()
+
+        @pl.when(jnp.logical_and(before, jnp.logical_not(first)))
+        def _():
+            pairs[to].wait_recv()
+            value = both(to)
+            came_sem = recv_sem.at[way, to]
+            remote(
+                came.at[way, to], came.at[way, to], send_sem.at[way, to], came_sem,
+                expert, partner,
+            ).wait_recv()
+            held[to] = (value + came[way, to].astype(jnp.float32)).astype(jnp.bfloat16)
+            line_copy(way, to).start()
+
+    for step in range(chips - 1):
+        hand_on(0, chips - 1 - step)
+        hand_on(1, step)
+
+    own_grads.wait()
+    for copy in grads_copies:
+        copy.wait_recv()
+    swap = remote(
+        grads_out.at[core], grads_out.at[core], swap_send, swap_recv, expert, partner
+    )
+    swap.start()
+    remote(
+        paired.at[chip], paired.at[chip], pair_send.at[chip], pair_recv.at[chip],
+        expert, partner,
+    ).wait_recv()
+    total[...] = both(chip)
+    for way, has in ((0, chip > 0), (1, chip < chips - 1)):
+
+        @pl.when(has)
+        def _(way=way):
+            remote(
+                came.at[way, chip], came.at[way, chip], send_sem.at[way, chip],
+                recv_sem.at[way, chip], expert, partner,
+            ).wait_recv()
+            total[...] += came[way, chip].astype(jnp.float32)
+
+    out[...] = total[...].astype(out.dtype)
+    for copy in grads_copies:
+        copy.wait_send()
+    swap.wait()
+    for to in range(chips):
+        pairs[to].wait_send()
+
+        @pl.when(chip < to)
+        def _(to=to):
+            line_copy(0, to).wait_send()
+
+        @pl.when(chip > to)
+        def _(to=to):
+            line_copy(1, to).wait_send()
+
+
+def reduce_rows(part, grads, experts, chips):
+    rows, width = part.shape[0] // (chips * CORES), part.shape[1]
+    vmem = pl.BlockSpec(memory_space=pltpu.VMEM)
+    dma = pltpu.SemaphoreType.DMA
+    return pl.pallas_call(
+        functools.partial(reduce_kernel, experts, chips),
+        out_shape=(
+            jax.ShapeDtypeStruct((rows, width), part.dtype),
+            jax.ShapeDtypeStruct((CORES, experts, chips) + grads.shape[1:], grads.dtype),
+        ),
+        in_specs=[vmem, vmem],
+        out_specs=(vmem, vmem),
+        scratch_shapes=[
+            pltpu.VMEM((chips, rows, width), part.dtype),
+            pltpu.VMEM((chips, rows, width), part.dtype),
+            pltpu.VMEM((2, chips, rows, width), part.dtype),
+            pltpu.VMEM((rows, width), jnp.float32),
+            dma((chips,)), dma((chips,)), dma((2, chips)), dma((2, chips)),
+            dma((experts * chips,)), dma((experts * chips,)), dma, dma, dma,
+        ],
+        compiler_params=pltpu.CompilerParams(
+            collective_id=1, has_side_effects=True, vmem_limit_bytes=VMEM_BYTES
+        ),
+    )(part, grads)
+
+
+def gather_kernel(
+    experts, chips, mine, left, out, shared, held, squares,
+    send_sem, recv_sem, pair_send, pair_recv, own_sem, share_send, share_recv,
+):
+    dps = chips * CORES
+    expert, dp = lax.axis_index("expert"), lax.axis_index("dp")
+    chip, core = dp // CORES, lax.rem(dp, CORES)
+    partner = chip * CORES + (1 - core)
+    rows, width = mine.shape
+    piece_rows = rows // PIECES
+    greet_all(experts, dps, expert, dp)
+
+    def place(of, core_of, piece):
+        start = (of * CORES + core_of) * rows + piece * piece_rows
+        return held.at[pl.ds(pl.multiple_of(start, 16), piece_rows)]
+
+    def part(piece):
+        return mine.at[pl.ds(piece * piece_rows, piece_rows)]
+
+    def line_copy(way, of, piece, src):
+        step = CORES if way == 0 else -CORES
+        return remote(
+            src, place(of, core, piece), send_sem.at[way, of, piece],
+            recv_sem.at[of, piece], expert, dp + step,
+        )
+
+    def pair_copy(of, piece, src):
+        return remote(
+            src, place(of, core, piece), pair_send.at[of, piece],
+            pair_recv.at[of, piece], expert, partner,
+        )
+
+    for piece in range(PIECES):
+
+        @pl.when(chip < chips - 1)
+        def _():
+            line_copy(0, chip, piece, part(piece)).start()
+
+        @pl.when(chip > 0)
+        def _():
+            line_copy(1, chip, piece, part(piece)).start()
+
+    own = pltpu.make_async_copy(
+        mine, held.at[pl.ds(pl.multiple_of(dp * rows, 16), rows)], own_sem
+    )
+    own.start()
+    for piece in range(PIECES):
+        pair_copy(chip, piece, part(piece)).start()
+
+    def multiply(of, begin):
+        for piece in range(PIECES):
+            remote(
+                place(of, 1 - core, piece), place(of, 1 - core, piece),
+                pair_send.at[of, piece], pair_recv.at[of, piece], expert, partner,
+            ).wait_recv()
+        depth = CORES * rows
+        some = pl.ds(pl.multiple_of(of * depth, 128), depth)
+
+        @pl.loop(0, width // TILE)
+        def _(tile):
+            columns = pl.ds(pl.multiple_of(tile * TILE, TILE), TILE)
+            product = jnp.dot(
+                left[:, some], held[some, columns], preferred_element_type=jnp.float32
+            )
+            if begin:
+                out[:, columns] = product
+            else:
+                out[:, columns] += product
+
+    def multiply_step(step):
+        @pl.when(chip >= step)
+        def _():
+            multiply(chip - step, False)
+
+        @pl.when(chip + step < chips)
+        def _():
+            multiply(chip + step, False)
+
+    for step in range(1, chips):
+        for piece in range(PIECES):
+            for way in (0, 1):
+                of = chip - step if way == 0 else chip + step
+                there = (of >= 0) if way == 0 else (of < chips)
+                goes_on = (chip < chips - 1) if way == 0 else (chip > 0)
+
+                @pl.when(there)
+                def _(of=of):
+                    remote(
+                        place(of, core, piece), place(of, core, piece),
+                        pair_send.at[of, piece], recv_sem.at[of, piece], expert, partner,
+                    ).wait_recv()
+
+                @pl.when(jnp.logical_and(there, goes_on))
+                def _(of=of, way=way):
+                    line_copy(way, of, piece, place(of, core, piece)).start()
+
+                @pl.when(there)
+                def _(of=of):
+                    pair_copy(of, piece, place(of, core, piece)).start()
+
+            if piece == 0:
+                if step == 1:
+                    own.wait()
+                    multiply(chip, True)
+                else:
+                    multiply_step(step - 1)
+    multiply_step(chips - 1)
+    value = out[...]
+    squares[...] = jnp.full(squares.shape, jnp.sum(value * value), jnp.float32)
+    copies = []
+    for offset in range(1, experts * dps):
+        copy = remote(
+            squares, shared.at[expert, dp], share_send.at[offset], share_recv.at[offset],
+            lax.rem(expert + offset // dps, experts), lax.rem(dp + offset % dps, dps),
+        )
+        copy.start()
+        copies.append(copy)
+    shared[expert, dp] = squares[...]
+    for of in range(chips):
+        for piece in range(PIECES):
+            pair_copy(of, piece, place(of, core, piece)).wait_send()
+
+            @pl.when(jnp.logical_and(chip >= of, chip < chips - 1))
+            def _(of=of):
+                line_copy(0, of, piece, place(of, core, piece)).wait_send()
+
+            @pl.when(jnp.logical_and(chip <= of, chip > 0))
+            def _(of=of):
+                line_copy(1, of, piece, place(of, core, piece)).wait_send()
+
+    for copy in copies:
+        copy.wait()
+
+
+def gather_multiply(mine, left, experts, chips):
+    rows, width = mine.shape
+    dps = chips * CORES
+    vmem = pl.BlockSpec(memory_space=pltpu.VMEM)
+    dma = pltpu.SemaphoreType.DMA
+    return pl.pallas_call(
+        functools.partial(gather_kernel, experts, chips),
+        out_shape=(
+            jax.ShapeDtypeStruct((rows, width), jnp.float32),
+            jax.ShapeDtypeStruct((experts, dps, 8, 128), jnp.float32),
+        ),
+        in_specs=[vmem, vmem],
+        out_specs=(vmem, vmem),
+        scratch_shapes=[
+            pltpu.VMEM((rows * dps, width), mine.dtype),
+            pltpu.VMEM((8, 128), jnp.float32),
+            dma((2, chips, PIECES)), dma((chips, PIECES)), dma((chips, PIECES)),
+            dma((chips, PIECES)), dma, dma((experts * dps,)), dma((experts * dps,)),
+        ],
+        compiler_params=pltpu.CompilerParams(
+            collective_id=2, has_side_effects=True, vmem_limit_bytes=VMEM_BYTES
+        ),
+    )(mine, left)
+
+
+def local_tokens(
+    experts, dps, acts, grad_out, routing_counts, left_basis, right_basis, first_moment, second_moment
+):
+    chips = dps // CORES
+    slot_count = acts.shape[2]
+    model_width, hidden_width = acts.shape[3], grad_out.shape[3]
+    own_width = model_width // dps
+    slot_index = lax.broadcasted_iota(jnp.int32, (experts, slot_count), 1)
+    live_slots = (slot_index < routing_counts[0][:, None])[..., None]
+    acts_live = jnp.where(live_slots, acts[0], jnp.zeros((), jnp.bfloat16))
+    grads_live = jnp.where(live_slots, grad_out[0], jnp.zeros((), jnp.bfloat16))
+    acts_cut = jnp.stack(
+        [acts_live[:, :, i * own_width : (i + 1) * own_width] for i in range(dps)]
+    )
+    token_acts = exchange(acts_cut, experts, chips)
+    token_acts = token_acts.reshape(-1, own_width)
+    right_block = right_basis[0]
+    left_rows = left_basis[0]
+    turned_acts = jnp.einsum(
+        "kc,tk->ct", left_rows, token_acts, preferred_element_type=jnp.float32
+    ).astype(jnp.bfloat16)
+    own_acts, token_grads = reduce_rows(turned_acts, grads_live, experts, chips)
+    token_grads = token_grads.reshape(-1, hidden_width)
+    turned_grads = jnp.dot(
+        token_grads, right_block, preferred_element_type=jnp.float32
+    ).astype(jnp.bfloat16)
+    rotated = jnp.dot(own_acts, turned_grads, preferred_element_type=jnp.float32)
+    first_new = BETA_ONE * first_moment[0] + (1.0 - BETA_ONE) * rotated
+    second_new = BETA_TWO * second_moment[0] + (1.0 - BETA_TWO) * rotated * rotated
+    direction = (first_new / (jnp.sqrt(second_new) + EPS_DIVIDE)).astype(jnp.bfloat16)
+    restored = jnp.einsum(
+        "kg,fg->kf", direction, right_block, preferred_element_type=jnp.float32
+    ).astype(jnp.bfloat16)
+    update, shared = gather_multiply(restored, left_rows, experts, chips)
+    cell_total = float(model_width * hidden_width)
+    norms = jnp.sqrt(jnp.sum(shared[:, :, 0, 0], axis=1) / cell_total + EPS_MEAN)
+    own_norm = lax.dynamic_index_in_dim(norms, lax.axis_index("expert"), keepdims=False)
+    mean_norm = jnp.mean(norms)
+    step_delta = (-update / jnp.maximum(own_norm, mean_norm)).astype(jnp.bfloat16)
+    return (step_delta[None], first_new[None], second_new[None], own_norm.reshape(1))
+
+
+def pick(experts, dps, *args):
+    acts, grad_out = args[0], args[1]
+    tokens = acts.shape[2] * experts * dps
+    rows = acts.shape[3] // dps
+    small = tokens <= grad_out.shape[3] and dps % CORES == 0 and rows % (16 * PIECES) == 0
+    small = small and CORES * rows % 128 == 0 and grad_out.shape[3] % TILE == 0
+    if small and acts.shape[0] == 1 and acts.shape[1] == experts:
+        return local_tokens(experts, dps, *args)
+    return local(*args)
+
+
 def solution(mesh):
     in_specs = (
         P(("expert", "dp"), None, None, None),
@@ -84,4 +520,5 @@
         P("expert", "dp", None),
         P("expert"),
     )
-    return jax.shard_map(local, mesh=mesh, in_specs=in_specs, out_specs=out_specs, check_vma=False)
+    run = functools.partial(pick, mesh.shape["expert"], mesh.shape["dp"])
+    return jax.shard_map(run, mesh=mesh, in_specs=in_specs, out_specs=out_specs, check_vma=False)

time: 313 us -> 190 us (0.61)
  Pallas kernels: 0 us -> 158 us
  waiting for transfers between devices: 134 us -> 0 us
  blocking collectives: 65 us -> 0 us
  local copies, waits for them, and re-layouts: 47.8 us -> 1.76 us
  matrix products: 31.1 us -> 15.6 us
  between operations: 16.3 us -> 2.05 us
  other arithmetic: 17.1 us -> 11.4 us
    pallas_call x0 -> x3, Pallas kernels: none -> 158 us  [the longest x1 77.3 us: gather_multiply(): pl.pallas_call(functools.partial(gather_kernel, experts, chips), out_shap...]
    unnamed x4 -> x0, waiting for transfers between devices: 70.9 us -> none
    all_gather x2 -> x0, waiting for transfers between devices: 63.6 us -> none  [the longest x1 63.6 us: local(): lax.all_gather(restored, 'dp', axis=0, tiled=True)]
    all_to_all x3 -> x0, blocking collectives: 39.1 us -> none  [the longest x1 18.9 us: local(): lax.all_to_all(came_acts, 'dp', split_axis=3, concat_axis=0, tiled=True)]
    unnamed x10 -> x11, local copies, waits for them, and re-layouts: 35.4 us -> 1.08 us
    psum x2 -> x0, blocking collectives: 25.9 us -> none  [the longest x1 14.7 us: local(): total_squares = lax.psum(squares, 'dp')]
    dot_general x4 -> x3, matrix products: 31.1 us -> 15.6 us  [the longest x1 5.99 us: local_tokens(): jnp.einsum('kc,tk->ct', left_rows, token_acts, preferred_element_type=jnp...]
    all_to_all x3 -> x0, local copies, waits for them, and re-layouts: 12.4 us -> none  [the longest x2 7.1 us: local(): lax.all_to_all(came_acts, 'dp', split_axis=3, concat_axis=0, tiled=True)]
  transfers between devices with their start and end apart: 3 -> 0, of which waited for: 2 -> 0; matrix products, arithmetic and copies ran while one was open for 12% -> 0% of each run, Pallas kernels for 0% -> 0%
where the time goes in v1:
time: 190 us; the launch traced here: 189 us
  Pallas kernels  158 us (83%)
  matrix products  15.6 us (8%)
  other arithmetic  11.4 us (6%)
  between operations  2.05 us (1%)
    pallas_call x1, Pallas kernels, gather_multiply(): pl.pallas_call(functools.partial(gather_kernel, experts, chips), out_shap...  77.3 us
    pallas_call x1, Pallas kernels, reduce_rows(): pl.pallas_call(functools.partial(reduce_kernel, experts, chips), out_shap...  59 us
    pallas_call x1, Pallas kernels, exchange(): pl.pallas_call(functools.partial(exchange_kernel, experts, chips), out_sh...  22.1 us
    broadcast_in_dim x1, other arithmetic, local_tokens(): second_new[None]  6.15 us
    dot_general x1, matrix products, local_tokens(): jnp.einsum('kc,tk->ct', left_rows, token_acts, preferred_element_type=jnp...  5.99 us
    dot_general x1, matrix products, local_tokens(): jnp.einsum('kg,fg->kf', direction, right_block, preferred_element_type=jn...  5.26 us
    dot_general x1, matrix products, local_tokens(): jnp.dot(own_acts, turned_grads, preferred_element_type=jnp.float32)  4.33 us

profile of v1, /device:TPU:0, one launch (start us, length us, event | category | flops | bytes accessed | tf_op | source)
XLA Modules:
  0.0 189.2 jit_solution(12607414617244013690)
XLA Ops:
  0.6 0.0 copy-start
  0.7 0.9 iota_compare_fusion
  1.5 1.6 bitcast_select_fusion.1.grads
  3.2 1.1 bitcast_select_fusion
  4.3 0.1 fusion.26
  4.4 0.1 fusion.24
  4.5 0.1 fusion.22
  4.6 0.1 fusion.20.acts
  4.7 0.0 copy-start.1
  4.7 0.8 copy-done.1
  5.5 22.1 %shard_map.102 = bf16[2,4,4,16,448]{4,3,2,1,0:T(8,128)(2,1)} custom-call(bf16[8,4,16,448]{3,2,1,0:T(8,128)(2,1)} %copy-done.1), custom_call_target="tpu_custom_call" | custom-call | tf_op jit(solution)/shard_map/pallas_call | solution.py:140
  27.6 6.0 %fusion.part = bf16[3584,512]{1,0:T(8,128)(2,1)} fusion(bf16[512,448]{1,0:T(8,128)(2,1)} %bitcast.80, bf16[1,448,3584]{2,1,0:T(8,128)(2,1)} %param.10), kind=kOutput, calls=%fused_computation.1 | convolution fusion | flops 1646002176 | bytes 7340032 | tf_op jit(solution)/shard_map/kc,tk->ct/dot_general | solution.py:472
  33.6 59.0 %shard_map.103 = (bf16[448,512]{1,0:T(8,128)(2,1)}, bf16[2,4,4,16,1024]{4,3,2,1,0:T(8,128)(2,1)}) custom-call(bf16[3584,512]{1,0:T(8,128)(2,1)} %fusion.part, bf16[4,16,1024]{2,1,0:T(8,128)(2,1)} %bitcast_select_fusion.1.grads), custom_call_target="tpu_custom_call" | custom-call | tf_op jit(solution)/shard_map/pallas_call | solution.py:273
  92.6 0.0 copy-done
  92.6 4.3 %fusion.13 = f32[448,1024]{1,0:T(8,128)} fusion(bf16[448,512]{1,0:T(8,128)(2,1)} %get-tuple-element.8, bf16[512,1024]{1,0:T(8,128)(2,1)} %bitcast.81, bf16[1,1024,1024]{2,1,0:T(8,128)(2,1)S(1)} %copy-done), kind=kOutput, calls=%fused_computation.13 | convolution fusion | flops 1544028160 | bytes 5439488 | tf_op jit(solution)/shard_map/dot_general | solution.py:480
  97.0 5.3 %fusion.9.mine = bf16[448,1024]{1,0:T(8,128)(2,1)} fusion(bf16[1,1024,1024]{2,1,0:T(8,128)(2,1)S(1)} %copy-done, f32[448,1024]{1,0:T(8,128)} %fusion.13, f32[1,448,1024]{2,1,0:T(8,128)} %param.12, f32[1,448,1024]{2,1,0:T(8,128)} %param.13), kind=kOutput, calls=%fused_computation.12 | convolution fusion | flops 944570368 | bytes 8519680 | tf_op jit(solution)/shard_map/kg,fg->kf/dot_general | solution.py:484
  102.2 77.3 %shard_map.104 = (f32[448,1024]{1,0:T(8,128)}, f32[4,8,8,128]{3,2,1,0:T(8,128)}) custom-call(bf16[448,1024]{1,0:T(8,128)(2,1)} %fusion.9.mine, bf16[448,3584]{1,0:T(8,128)(2,1)} %bitcast.79), custom_call_target="tpu_custom_call" | custom-call | tf_op jit(solution)/shard_map/pallas_call | solution.py:434
  179.5 1.0 slice_reduce_fusion
  180.5 0.6 fusion.34
  181.8 0.6 dynamic_slice.4
  183.1 6.2 %fusion.18 = (f32[1,448,1024]{2,1,0:T(8,128)}, f32[1,448,1024]{2,1,0:T(8,128)}, bf16[1,448,1024]{2,1,0:T(8,128)(2,1)}) fusion(f32[448,1024]{1,0:T(8,128)} %fusion.13, f32[1,448,1024]{2,1,0:T(8,128)} %param.13, f32[1,448,1024]{2,1,0:T(8,128)} %param.12, f32[]{:T(128)S(6)} %max.3, f32[448,1024]{1,0:T(8,128)} %get-tuple-element.10), kind=kLoop, calls=%fused_computation.17 | loop fusion | flops 4587520 | bytes 11927556 | tf_op jit(solution)/shard_map/broadcast_in_dim | solution.py:493
  (4 shorter events, 0.0 us)
Async XLA Ops:
  0.6 92.0 %copy-start = (bf16[1,1024,1024]{2,1,0:T(8,128)(2,1)S(1)}, bf16[1,1024,1024]{2,1,0:T(8,128)(2,1)}, u32[]{:S(2)}) copy-start(bf16[1,1024,1024]{2,1,0:T(8,128)(2,1)} %param.11) | copy-start | bytes 6291460
  4.7 0.8 copy-start.1
